TPU v7x, 512 devices: a whole 4x8x8 slice. The times are simulated.
512 devices in a mesh: tm: 128 (over y, z, x_hi), series: 4 (over x_lo, core).
Axes of the slice: x: 4 (x_hi: 2, x_lo: 2; x = x_hi * 2 + x_lo), y: 8, z: 8, core: 2. Of those that a mesh axis runs over, the one named last changes fastest.
Arguments:
- returns: float32 [32768, 8192], P('tm', 'series'), may hold values from -40 to 40
- sector: int32 [8192], P('series'), may hold values from 0 to 511, as said below
Outputs:
- shrunk_variance: float32 [32768, 8192], P('tm', 'series')
Inputs may be any that keep to these rules, and one draw needn't show every extreme that they name: `sector`: sectors differ widely in size; some sectors may hold no series.
All inputs are finite; a program needn't handle non-finite values.
Results may differ from a plain program's by a relative error of at most 0.0003.
Values sent between devices are 32-bit elements; how exact they have to be, the bound alone decides.
A program may use at most 64 MiB of HBM per device.

v0:
```python
import functools

import jax
import jax.numpy as jnp
from jax import lax
from jax.sharding import Mesh
from jax.sharding import PartitionSpec as P

W = 64
SECTORS = 512
TM = ("tm_0", "tm_1", "tm_2")


ridge_rate = 0.05
shrink_weight = 0.3
highest = lax.Precision.HIGHEST


def from_everyone(array, axis):
    size = lax.axis_size(axis)
    return lax.all_to_all(
        jnp.broadcast_to(array[None], (size, *array.shape)), axis, 0, 0, tiled=True
    )


def taken_together(array, axis):
    return from_everyone(array, axis).sum(axis=0)


def packed_total(arrays, axis):
    line, at, gathered = (jnp.concatenate([a.reshape(-1) for a in arrays]), 0, [])
    so_far = taken_together(line, axis)
    for a in arrays:
        gathered.append(so_far[at : at + a.size].reshape(a.shape))
        at += a.size
    return tuple(gathered)


def shifted(value, axis, steps):
    count = lax.axis_size(axis)
    leading, last = (max(0, -steps), min(count, count - steps))
    return lax.ppermute(value, axis, [(source, source + steps) for source in range(leading, last)])


def over_axes(array, axes):
    return functools.reduce(lax.psum, axes, array)


def sector_table(sector):
    labels = jnp.arange(SECTORS, dtype=jnp.int32)
    return (sector[:, None] == labels[None, :]).astype(jnp.float32)


def band_matrix(rows):
    row_pos = jnp.arange(rows, dtype=jnp.int32)[:, None]
    col_pos = jnp.arange(rows + W - 1, dtype=jnp.int32)[None, :]
    return ((col_pos >= row_pos) & (col_pos < row_pos + W)).astype(jnp.float32)


def window_variance(ext_returns, ext_factor, first_step):
    rows = ext_returns.shape[0] - (W - 1)
    series_width = ext_returns.shape[1]
    stacked = jnp.concatenate(
        [
            ext_returns,
            ext_factor,
            ext_returns * ext_returns,
            ext_factor * ext_factor,
            ext_returns * ext_factor,
        ],
        axis=1,
    )
    moments = jnp.dot(
        band_matrix(rows), stacked, precision=highest, preferred_element_type=jnp.float32
    )
    sum_ret = moments[:, :series_width]
    sum_fac = moments[:, series_width : 2 * series_width]
    sum_rr = moments[:, 2 * series_width : 3 * series_width]
    sum_ff = moments[:, 3 * series_width : 4 * series_width]
    sum_rf = moments[:, 4 * series_width :]
    steps_seen = jnp.minimum(first_step + jnp.arange(rows, dtype=jnp.int32) + 1, W).astype(
        jnp.float32
    )[:, None]
    centred_rr = sum_rr - sum_ret * sum_ret / steps_seen
    centred_ff = sum_ff - sum_fac * sum_fac / steps_seen
    centred_rf = sum_rf - sum_ret * sum_fac / steps_seen
    return (
        centred_rr - centred_rf * centred_rf / (centred_ff + ridge_rate * steps_seen)
    ) / steps_seen


def local(returns, sector):
    time_rows = returns.shape[0]
    table = sector_table(sector)
    part_sums = jnp.dot(returns, table, precision=highest, preferred_element_type=jnp.float32)
    part_counts = jnp.sum(table, axis=0)
    sums, counts = packed_total((part_sums, part_counts), "series")
    means = sums / jnp.maximum(counts, 1.0)[None, :]
    factor = jnp.dot(means, table.T, precision=highest, preferred_element_type=jnp.float32)
    prior_ret, prior_means = shifted(
        (returns[time_rows - (W - 1) :], means[time_rows - (W - 1) :]), TM, 1
    )
    prior_fac = jnp.dot(prior_means, table.T, precision=highest, preferred_element_type=jnp.float32)
    ext_returns = jnp.concatenate([prior_ret, returns], axis=0)
    ext_factor = jnp.concatenate([prior_fac, factor], axis=0)
    first_step = lax.axis_index(TM) * time_rows
    variance = window_variance(ext_returns, ext_factor, first_step)
    part_totals = jnp.dot(
        jnp.sum(variance, axis=0)[None, :],
        table,
        precision=highest,
        preferred_element_type=jnp.float32,
    )[0]
    series_totals = taken_together(part_totals, "series")
    totals = over_axes(series_totals, TM)
    all_steps = time_rows * lax.axis_size(TM)
    sector_mean = totals / (all_steps * jnp.maximum(counts, 1.0))
    pooled = jnp.dot(
        sector_mean[None, :], table.T, precision=highest, preferred_element_type=jnp.float32
    )
    return (1.0 - shrink_weight) * variance + shrink_weight * pooled


def solution(mesh):
    torus = Mesh(
        mesh.devices.reshape(8, 8, 2, mesh.shape["series"]), ("tm_0", "tm_1", "tm_2", "series")
    )
    in_specs = (P(TM, "series"), P("series"))
    out_specs = P(TM, "series")
    return jax.shard_map(local, mesh=torus, in_specs=in_specs, out_specs=out_specs, check_vma=False)
```

profile of v0, /device:TPU:4, one launch (start us, length us, event | category | flops | bytes accessed | tf_op | source)
XLA Modules:
  0.0 153.4 jit_solution(2079003674793114173)
XLA Ops:
  0.0 1.3 convert_reduce_fusion
  1.3 4.4 %fusion.19 = f32[256,512]{0,1:T(8,128)S(1)} fusion(f32[256,2048]{1,0:T(8,128)} %param.2, s32[2048]{0:T(1024)} %param.3), kind=kOutput, calls=%fused_computation.29 | convolution fusion | flops 3223322624 | bytes 2629632 | tf_op jit(solution)/shard_map/dot_general | solution.py:95
  5.7 0.2 copy.5
  5.9 0.1 copy.12
  6.1 3.5 %broadcast_in_dim.4 = f32[4,1,131584]{2,1,0:T(1,128)} broadcast(f32[131584]{0:T(1024)S(1)} %pad_maximum_fusion.2), dimensions={2} | broadcast | bytes 2631680 | tf_op jit(solution)/shard_map/broadcast_in_dim | solution.py:22
  9.5 0.0 copy-start
  9.5 4.6 %all-to-all-start = ((f32[4,1,131584]{2,1,0:T(1,128)}), f32[4,1,131584]{2,1,0:T(1,128)}, u32[]{:S(2)}, u32[]{:S(2)}) async-start(f32[4,1,131584]{2,1,0:T(1,128)} %broadcast_in_dim.4), calls=%async_computation | async-start | bytes 4210688 | tf_op jit(solution)/shard_map/all_to_all | solution.py:21
  14.2 0.0 copy-done
  14.2 4.2 %collective-permute-start = (f32[63,2048]{1,0:T(8,128)S(1)}, f32[63,2048]{1,0:T(8,128)S(1)}, u32[]{:S(2)}, u32[]{:S(2)}) collective-permute-start(f32[63,2048]{1,0:T(8,128)S(1)} %slice.37), channel_id=1, source_target_pairs={{0,4},{4,8},{8,12},{12,16},{16,20},{20,24},{24,28},{28,32},{32,36}... | collective-permute-start | bytes 1548296 | tf_op jit(solution)/shard_map/ppermute | solution.py:42
  18.5 36.8 %collective-permute-done = f32[63,2048]{1,0:T(8,128)S(1)} collective-permute-done((f32[63,2048]{1,0:T(8,128)S(1)}, f32[63,2048]{1,0:T(8,128)S(1)}, u32[]{:S(2)}, u32[]{:S(2)}) %collective-permute-start) | collective-permute-done | bytes 516128 | tf_op jit(solution)/shard_map/ppermute | solution.py:42
  55.3 1.8 %fusion.17 = f32[319,10240]{1,0:T(8,128)} fusion(f32[256,2048]{1,0:T(8,128)S(1)} %copy-done, f32[63,2048]{1,0:T(8,128)S(1)} %collective-permute-done), kind=kLoop, calls=%fused_computation.27 | loop fusion | flops 653311 | bytes 5234688
  57.2 0.0 copy-start.1
  57.2 0.0 all-to-all-done
  57.2 5.4 %reduce_sum.37 = f32[131584]{0:T(1024)S(1)} reduce(f32[4,1,131584]{2,1,0:T(1,128)} %all-to-all-done, f32[]{:T(128)} %constant.7.clone.1), dimensions={0,1}, to_apply=%region_1.0 | reduce | flops 394752 | bytes 2631684 | tf_op jit(solution)/shard_map/reduce_sum | solution.py:27
  62.6 0.8 slice.47
  63.5 2.0 %slice.39 = f32[256,512]{1,0:T(8,128)} reshape(f32[131072]{0:T(1024)} %slice.47) | data formatting | bytes 1048576 | tf_op jit(solution)/shard_map/slice | solution.py:34
  65.4 1.1 broadcast_divide_fusion
  66.5 2.1 %collective-permute-start.1 = (f32[63,512]{1,0:T(8,128)S(1)}, f32[63,512]{1,0:T(8,128)S(1)}, u32[]{:S(2)}, u32[]{:S(2)}) collective-permute-start(f32[63,512]{1,0:T(8,128)S(1)} %slice.49), channel_id=1, source_target_pairs={{0,4},{4,8},{8,12},{12,16},{16,20},{20,24},{24,28},{28,32},{32,36}... | collective-permute-start | bytes 387080 | tf_op jit(solution)/shard_map/ppermute | solution.py:42
  68.7 0.0 copy-done.1
  68.7 2.5 %fusion.2 = f32[256,2048]{1,0:T(8,128)S(1)} fusion(f32[256,512]{1,0:T(8,128)S(1)} %broadcast_divide_fusion, s32[2048]{0:T(1024)S(1)} %copy-done.1), kind=kOutput, calls=%fused_computation.4 | convolution fusion | flops 3222274048 | bytes 2629632 | tf_op jit(solution)/shard_map/dot_general | solution.py:99
  71.2 4.0 %collective-permute-done.1 = f32[63,512]{1,0:T(8,128)S(1)} collective-permute-done((f32[63,512]{1,0:T(8,128)S(1)}, f32[63,512]{1,0:T(8,128)S(1)}, u32[]{:S(2)}, u32[]{:S(2)}) %collective-permute-start.1) | collective-permute-done | bytes 129056 | tf_op jit(solution)/shard_map/ppermute | solution.py:42
  75.2 2.4 %fusion.3 = f32[63,2048]{1,0:T(8,128)S(1)} fusion(f32[63,512]{1,0:T(8,128)S(1)} %collective-permute-done.1, s32[2048]{0:T(1024)S(1)} %copy-done.1), kind=kOutput, calls=%fused_computation.5 | convolution fusion | flops 793772032 | bytes 653312 | tf_op jit(solution)/shard_map/dot_general | solution.py:103
  77.7 1.8 %fusion.18 = f32[319,10240]{1,0:T(8,128)} fusion(f32[319,10240]{1,0:T(8,128)} %fusion.17, f32[256,2048]{1,0:T(8,128)S(1)} %fusion.2, f32[63,2048]{1,0:T(8,128)S(1)} %fusion.3), kind=kLoop, calls=%fused_computation.28 | loop fusion | flops 653312 | bytes 5234688
  79.5 2.0 %multiply_dynamic-update-slice_fusion.2 = f32[319,10240]{1,0:T(8,128)} fusion(f32[319,10240]{1,0:T(8,128)} %fusion.18, f32[256,2048]{1,0:T(8,128)S(1)} %copy-done, f32[63,2048]{1,0:T(8,128)S(1)} %collective-permute-done), kind=kLoop, calls=%fused_computation.11 | loop fusion | flops 1306624 | bytes 5234688
  81.5 1.9 %multiply_dynamic-update-slice_fusion.1 = f32[319,10240]{1,0:T(8,128)} fusion(f32[319,10240]{1,0:T(8,128)} %multiply_dynamic-update-slice_fusion.2, f32[256,2048]{1,0:T(8,128)S(1)} %fusion.2, f32[63,2048]{1,0:T(8,128)S(1)} %fusion.3), kind=kLoop, calls=%fused_computation.10 | loop fusion | flops 1306624 | bytes 5234688
  83.4 2.3 %multiply_dynamic-update-slice_fusion = f32[319,10240]{1,0:T(8,128)} fusion(f32[319,10240]{1,0:T(8,128)} %multiply_dynamic-update-slice_fusion.1, f32[256,2048]{1,0:T(8,128)S(1)} %copy-done, f32[63,2048]{1,0:T(8,128)S(1)} %collective-permute-done, f32[256,2048]{1,0:T(8,128)S(1)} %fusion.2, f32[63,2048]{1,0:T(8,128)S(1)} %fusion.3), kind=kLoop, calls=%fused_computation.9 | loop fusion | flops 1959936 | bytes 7847936 | tf_op jit(solution)/shard_map/concatenate | solution.py:63
  85.7 12.1 %fusion.23 = f32[256,10240]{1,0:T(8,128)S(1)} fusion(f32[319,10240]{1,0:T(8,128)} %multiply_dynamic-update-slice_fusion, s32[256]{0:T(256)S(1)} %iota_add_fusion), kind=kOutput, calls=%fused_computation.34 | convolution fusion | flops 10035117056 | bytes 23553024 | tf_op jit(solution)/shard_map/dot_general | solution.py:73
  97.8 1.6 %fusion.26 = (f32[2048]{0:T(1024)S(1)}, f32[256,2048]{1,0:T(8,128)S(1)}) fusion(f32[256]{0:T(256)S(1)} %broadcast_multiply_fusion.1, f32[256,10240]{1,0:T(8,128)S(1)} %fusion.23, f32[256]{0:T(256)S(1)} %minimum_convert_fusion), kind=kLoop, calls=%fused_computation.43 | loop fusion | flops 7862272 | bytes 12593152 | tf_op jit(solution)/shard_map/reduce_sum | solution.py:109
  99.4 1.4 fusion.1
  100.8 6.8 %all_to_all.12 = f32[4,1,512]{2,1,0:T(1,128)S(1)} all-to-all(f32[4,1,512]{2,1,0:T(1,128)S(1)} %broadcast_in_dim.5), channel_id=1, replica_groups=mesh['tm_0'=8,'tm_1'=8,'tm_2'=2,'series'=4] {'series'}, dimensions={0} | all-to-all | bytes 16384 | tf_op jit(solution)/shard_map/all_to_all | solution.py:21
  107.6 14.2 %psum.21 = f32[512]{0:T(512)S(1)} all-reduce(f32[512]{0:T(512)S(1)} %reduce_sum.39), channel_id=1, replica_groups=mesh['tm_0'=8,'tm_1'=8,'tm_2'=2,'series'=4] {'tm_0'}, use_global_device_ids=true, to_apply=%region_4.0 | all-reduce | flops 512 | bytes 4096 | tf_op jit(solution)/shard_map/psum | solution.py:46
  121.8 21.3 %psum.22 = f32[512]{0:T(512)S(1)} all-reduce(f32[512]{0:T(512)S(1)} %psum.21), channel_id=1, replica_groups=mesh['tm_0'=8,'tm_1'=8,'tm_2'=2,'series'=4] {'tm_1'}, use_global_device_ids=true, to_apply=%region_5.0 | all-reduce | flops 512 | bytes 4096 | tf_op jit(solution)/shard_map/psum | solution.py:46
  143.1 6.4 %psum.23 = f32[512]{0:T(512)S(1)} all-reduce(f32[512]{0:T(512)S(1)} %psum.22), channel_id=1, replica_groups=mesh['tm_0'=8,'tm_1'=8,'tm_2'=2,'series'=4] {'tm_2'}, use_global_device_ids=true, to_apply=%region_6.0 | all-reduce | flops 512 | bytes 4096 | tf_op jit(solution)/shard_map/psum | solution.py:46
  149.5 2.2 %fusion = f32[1,2048]{1,0:T(1,128)S(1)} fusion(f32[512,1]{0,1:T(1,128)S(1)} %bitcast.18, s32[2048]{0:T(1024)S(1)} %copy-done.1), kind=kOutput, calls=%fused_computation.2 | convolution fusion | flops 13631488 | bytes 18432 | tf_op jit(solution)/shard_map/dot_general | solution.py:118
  151.7 1.7 %multiply_add_fusion = f32[256,2048]{1,0:T(8,128)} fusion(f32[256,2048]{1,0:T(8,128)S(1)} %get-tuple-element.6, f32[2048]{0:T(1024)S(1)} %broadcast_multiply_fusion), kind=kLoop, calls=%fused_computation.21 | loop fusion | flops 1048576 | bytes 4202496 | tf_op jit(solution)/shard_map/add | solution.py:121
  (11 shorter events, 0.2 us)
Async XLA Ops:
  9.5 4.6 %copy-start = (f32[256,2048]{1,0:T(8,128)S(1)}, f32[256,2048]{1,0:T(8,128)}, u32[]{:S(2)}) copy-start(f32[256,2048]{1,0:T(8,128)} %param.2) | copy-start | bytes 6291460
  9.5 47.6 %all-to-all-start = ((f32[4,1,131584]{2,1,0:T(1,128)}), f32[4,1,131584]{2,1,0:T(1,128)}, u32[]{:S(2)}, u32[]{:S(2)}) async-start(f32[4,1,131584]{2,1,0:T(1,128)} %broadcast_in_dim.4), calls=%async_computation | async-start | bytes 4210688 | tf_op jit(solution)/shard_map/all_to_all | solution.py:21
  14.2 41.1 %collective-permute-start = (f32[63,2048]{1,0:T(8,128)S(1)}, f32[63,2048]{1,0:T(8,128)S(1)}, u32[]{:S(2)}, u32[]{:S(2)}) collective-permute-start(f32[63,2048]{1,0:T(8,128)S(1)} %slice.37), channel_id=1, source_target_pairs={{0,4},{4,8},{8,12},{12,16},{16,20},{20,24},{24,28},{28,32},{32,36}... | collective-permute-start | bytes 1548296 | tf_op jit(solution)/shard_map/ppermute | solution.py:42
  57.2 11.5 %copy-start.1 = (s32[2048]{0:T(1024)S(1)}, s32[2048]{0:T(1024)}, u32[]{:S(2)}) copy-start(s32[2048]{0:T(1024)} %param.3) | copy-start | bytes 24580
  66.5 8.7 %collective-permute-start.1 = (f32[63,512]{1,0:T(8,128)S(1)}, f32[63,512]{1,0:T(8,128)S(1)}, u32[]{:S(2)}, u32[]{:S(2)}) collective-permute-start(f32[63,512]{1,0:T(8,128)S(1)} %slice.49), channel_id=1, source_target_pairs={{0,4},{4,8},{8,12},{12,16},{16,20},{20,24},{24,28},{28,32},{32,36}... | collective-permute-start | bytes 387080 | tf_op jit(solution)/shard_map/ppermute | solution.py:42
where the time goes:
time: 154 us; the launch traced here: 153 us
  blocking collectives  48.7 us (32%)
  waiting for transfers between devices  40.9 us (27%)
  matrix products  25 us (16%)
  other arithmetic  21 us (14%)
  starting transfers between devices  11 us (7%)
  local copies, waits for them, and re-layouts  6.67 us (4%)
    psum x3, blocking collectives, over_axes(): return functools.reduce(lax.psum, axes, array)  41.9 us
    ppermute x2, waiting for transfers between devices, shifted(): lax.ppermute(value, axis, [(source, source + steps) for source in range(l...  40.9 us
    dot_general x1, matrix products, window_variance(): jnp.dot(band_matrix(rows), stacked, precision=highest, preferred_element_...  12.1 us
    unnamed x4, other arithmetic  7.56 us
    all_to_all x1, blocking collectives, from_everyone(): lax.all_to_all(jnp.broadcast_to(array[None], (size, *array.shape)), axis,...  6.79 us
    ppermute x2, starting transfers between devices, shifted(): lax.ppermute(value, axis, [(source, source + steps) for source in range(l...  6.32 us
    reduce_sum x2, other arithmetic, taken_together(): return from_everyone(array, axis).sum(axis=0)  5.46 us
    all_to_all x1, starting transfers between devices, from_everyone(): lax.all_to_all(jnp.broadcast_to(array[None], (size, *array.shape)), axis,...  4.63 us
  transfers between devices with their start and end apart: 3, of which 2 were waited for; matrix products, arithmetic and copies ran while one was open for 3% of the time, Pallas kernels for 0%

commit v1 on v0

v1 whole, which is shorter than its diff:
```python
import jax
import jax.numpy as jnp
from jax import lax
from jax.experimental import pallas as pl
from jax.experimental.pallas import tpu as pltpu
from jax.sharding import Mesh
from jax.sharding import PartitionSpec as P

W = 64
SECTORS = 512
AXES = ("y", "z", "xh", "xl", "c")
MESH_IDS = pl.DeviceIdType.MESH

ridge_rate = 0.05
shrink_weight = 0.3

COUNT_ROWS = 8
CHUNK = 256
EARLY = 3


def split3(value):
    hi = value.astype(jnp.bfloat16)
    rest = value - hi.astype(jnp.float32)
    mid = rest.astype(jnp.bfloat16)
    lo = (rest - mid.astype(jnp.float32)).astype(jnp.bfloat16)
    return jnp.concatenate([hi, mid, lo], axis=0)


def joined3(value):
    rows = value.shape[0] // 3
    return value[:rows] + value[rows : 2 * rows] + value[2 * rows :]


def windowed(value):
    shift = 1
    while shift < W:
        value = value + pltpu.roll(value, shift, 0)
        shift *= 2
    return value[W:]


def window_variance(ret, fac, steps, inv_steps):
    sum_ret = windowed(ret)
    sum_fac = windowed(fac)
    sum_rr = windowed(ret * ret)
    sum_ff = windowed(fac * fac)
    sum_rf = windowed(ret * fac)
    mean_fac = sum_fac * inv_steps
    centred_rr = sum_rr - sum_ret * sum_ret * inv_steps
    centred_ff = sum_ff - sum_fac * mean_fac
    centred_rf = sum_rf - sum_ret * mean_fac
    return (
        centred_rr - centred_rf * centred_rf / (centred_ff + ridge_rate * steps)
    ) * inv_steps


def by_eights(value):
    total = value[0:8]
    for row in range(8, value.shape[0], 8):
        total = total + value[row : row + 8]
    return total


def remote(src, dst, send, recv, device):
    return pltpu.make_async_remote_copy(
        src_ref=src,
        dst_ref=dst,
        send_sem=send,
        recv_sem=recv,
        device_id=device,
        device_id_type=MESH_IDS,
    )


def make_kernel(sizes, time_rows, series):
    n_y, n_z = sizes["y"], sizes["z"]
    half = time_rows // 2
    chunks = series // CHUNK
    tail = W // 2

    def kernel(
        ret_hbm,
        sector_ref,
        var_hbm,
        pooled_ref,
        ret,
        fac,
        table,
        part,
        mine,
        from_core,
        from_pair,
        means,
        prior,
        var,
        col,
        gx,
        gy,
        gz,
        load_sem,
        halo_send,
        halo_recv,
        ex_send,
        ex_recv,
        pm_send,
        pm_recv,
        out_sem,
        gx_send,
        gx_recv,
        gy_send,
        gy_recv,
        gz_send,
        gz_recv,
    ):
        y, z = lax.axis_index("y"), lax.axis_index("z")
        xh, xl, c = lax.axis_index("xh"), lax.axis_index("xl"), lax.axis_index("c")
        block = (y * n_z + z) * 2 + xh
        n_blocks = n_y * n_z * 2

        def place(b):
            b = lax.rem(b + n_blocks, n_blocks)
            return {"y": b // (2 * n_z), "z": lax.rem(b // 2, n_z), "xh": lax.rem(b, 2)}

        following, previous = place(block + 1), place(block - 1)
        core = {"c": 1 - c}
        pair = {"xl": 1 - xl}

        def x_peer(d):
            p = lax.rem(xh * 4 + xl * 2 + c + d, 8)
            return {"xh": p // 4, "xl": lax.rem(p // 2, 2), "c": lax.rem(p, 2)}

        def y_peer(d):
            return {"y": lax.rem(y + d, n_y)}

        def z_peer(d):
            return {"z": lax.rem(z + d, n_z)}

        peers = [following, previous]
        peers += [x_peer(d) for d in range(1, 8)]
        peers += [y_peer(d) for d in range(1, n_y)]
        peers += [z_peer(d) for d in range(1, n_z)]
        barrier = pltpu.get_barrier_semaphore()
        for peer in peers:
            pl.semaphore_signal(barrier, inc=1, device_id=peer, device_id_type=MESH_IDS)

        loads = [
            pltpu.make_async_copy(
                ret_hbm.at[time_rows - W :], ret.at[time_rows:], load_sem.at[0]
            ),
            pltpu.make_async_copy(
                ret_hbm.at[: time_rows - W], ret.at[W:time_rows], load_sem.at[1]
            ),
        ]
        for load in loads:
            load.start()

        @pl.loop(0, chunks)
        def _(i):
            at = pl.multiple_of(i * CHUNK, CHUNK)
            labels = lax.broadcasted_iota(jnp.int32, (SECTORS, CHUNK), 0)
            hit = labels == sector_ref[:, pl.ds(at, CHUNK)]
            table[:, pl.ds(at, CHUNK)] = hit.astype(jnp.float32).astype(jnp.bfloat16)

        loads[0].wait()
        pl.semaphore_wait(barrier, len(peers))

        def halo(i):
            at = pl.multiple_of(i * CHUNK, CHUNK)
            return remote(
                ret.at[time_rows:, pl.ds(at, CHUNK)],
                ret.at[:W, pl.ds(at, CHUNK)],
                halo_send.at[i],
                halo_recv.at[i],
                following,
            )

        for i in range(EARLY):
            halo(i).start()
        loads[1].wait()

        def partial_sums(which, into):
            first = pl.multiple_of(W + which * half, W)
            into[...] = jnp.zeros_like(into)

            @pl.loop(0, chunks)
            def _(i):
                at = pl.multiple_of(i * CHUNK, CHUNK)
                lhs = jnp.concatenate(
                    [
                        split3(ret[pl.ds(first, half), pl.ds(at, CHUNK)]),
                        jnp.ones((2 * COUNT_ROWS, CHUNK), jnp.bfloat16),
                    ],
                    axis=0,
                )
                got = lax.dot_general(
                    lhs,
                    table[:, pl.ds(at, CHUNK)],
                    (((1,), (1,)), ((), ())),
                    preferred_element_type=jnp.float32,
                )
                into[:half] += joined3(got[: 3 * half])
                into[half:] += got[3 * half : 3 * half + COUNT_ROWS]

        partial_sums(1 - c, part)
        to_core = remote(part, from_core, ex_send.at[0], ex_recv.at[0], core)
        to_core.start()
        partial_sums(c, mine)
        to_core.wait_recv()
        mine[...] = mine[...] + from_core[...]
        to_pair = remote(mine, from_pair, ex_send.at[1], ex_recv.at[1], pair)
        to_pair.start()
        to_pair.wait_recv()
        for i in range(EARLY, chunks):
            halo(i).start()

        own = pl.ds(pl.multiple_of(c * half, half), half)
        counts = jnp.maximum(mine[half : half + 1] + from_pair[half : half + 1], 1.0)
        means[own] = (mine[:half] + from_pair[:half]) / counts
        share = remote(means.at[own], means.at[own], ex_send.at[2], ex_recv.at[2], core)
        share.start()
        share.wait_recv()

        low = pl.multiple_of(c * tail, tail)
        pm_rows = prior.at[pl.ds(low, tail)]
        pm_on = remote(
            means.at[pl.ds(time_rows - W + low, tail)],
            pm_rows,
            pm_send.at[0],
            pm_recv.at[0],
            following,
        )
        pm_on.start()

        full = jnp.float32(W)

        def out_copy(i, first, rows, slot):
            at = pl.multiple_of(i * CHUNK, CHUNK)
            return pltpu.make_async_copy(
                var.at[pl.ds(first, rows), pl.ds(at, CHUNK)],
                var_hbm.at[pl.ds(first, rows), pl.ds(at, CHUNK)],
                out_sem.at[slot, i],
            )

        @pl.loop(0, chunks)
        def _(i):
            at = pl.multiple_of(i * CHUNK, CHUNK)
            got = jnp.dot(
                split3(means[...]),
                table[:, pl.ds(at, CHUNK)],
                preferred_element_type=jnp.float32,
            )
            fac[pl.ds(W, time_rows), pl.ds(at, CHUNK)] = joined3(got)
            for s in range(CHUNK // 128):
                lanes = pl.ds(at + s * 128, 128)
                value = window_variance(
                    ret[pl.ds(W, time_rows), lanes],
                    fac[pl.ds(W, time_rows), lanes],
                    full,
                    1.0 / full,
                )
                col[:, lanes] = by_eights(value)
                var[pl.ds(W, time_rows - W), lanes] = (1.0 - shrink_weight) * value
            out_copy(i, W, time_rows - W, 0).start()

        pm_on.wait_recv()
        pm_share = remote(pm_rows, pm_rows, pm_send.at[1], pm_recv.at[1], core)
        pm_share.start()
        pm_share.wait_recv()
        started = block > 0

        @pl.loop(0, chunks)
        def _(i):
            at = pl.multiple_of(i * CHUNK, CHUNK)
            got = jnp.dot(
                split3(jnp.where(started, prior[...], 0.0)),
                table[:, pl.ds(at, CHUNK)],
                preferred_element_type=jnp.float32,
            )
            fac[pl.ds(0, W), pl.ds(at, CHUNK)] = joined3(got)

        seen = lax.broadcasted_iota(jnp.int32, (W, 128), 0) + 1 + block * time_rows
        steps = jnp.minimum(seen, W).astype(jnp.float32)
        inv_steps = 1.0 / steps
        gx[0] = jnp.zeros((8, SECTORS), jnp.float32)

        @pl.loop(0, chunks)
        def _(i):
            at = pl.multiple_of(i * CHUNK, CHUNK)
            halo(i).wait_recv()
            for s in range(CHUNK // 128):
                lanes = pl.ds(at + s * 128, 128)
                before = jnp.where(started, ret[pl.ds(0, W), lanes], 0.0)
                value = window_variance(
                    jnp.concatenate([before, ret[pl.ds(W, W), lanes]], axis=0),
                    fac[pl.ds(0, 2 * W), lanes],
                    steps,
                    inv_steps,
                )
                col[:, lanes] += by_eights(value)
                var[pl.ds(0, W), lanes] = (1.0 - shrink_weight) * value
            out_copy(i, 0, W, 1).start()
            got = lax.dot_general(
                split3(col[:, pl.ds(at, CHUNK)]),
                table[:, pl.ds(at, CHUNK)],
                (((1,), (1,)), ((), ())),
                preferred_element_type=jnp.float32,
            )
            gx[0] += joined3(got)

        def exchange(buf, peer_of, send, recv, count, total):
            buf[0] = jnp.broadcast_to(total, (8, SECTORS))
            copies = [
                remote(
                    buf.at[0, pl.ds(0, 1)],
                    buf.at[d, pl.ds(0, 1)],
                    send.at[d],
                    recv.at[d],
                    peer_of(d),
                )
                for d in range(1, count)
            ]
            for copy in copies:
                copy.start()
            for copy in copies:
                copy.wait_recv()
            total = buf[0, 0:1]
            for d in range(1, count):
                total = total + buf[d, 0:1]
            for copy in copies:
                copy.wait_send()
            return total

        total = jnp.sum(gx[0], axis=0, keepdims=True)
        total = exchange(gx, x_peer, gx_send, gx_recv, 8, total)
        total = exchange(gy, y_peer, gy_send, gy_recv, n_y, total)
        total = exchange(gz, z_peer, gz_send, gz_recv, n_z, total)

        all_steps = float(time_rows * n_blocks)
        sector_mean = total / (all_steps * counts)
        got = jnp.dot(
            split3(jnp.broadcast_to(shrink_weight * sector_mean, (8, SECTORS))),
            table[...],
            preferred_element_type=jnp.float32,
        )
        pooled_ref[...] = joined3(got)[0:1]

        for i in range(chunks):
            out_copy(i, W, time_rows - W, 0).wait()
            out_copy(i, 0, W, 1).wait()
            halo(i).wait_send()
        for copy in (to_core, to_pair, share, pm_on, pm_share):
            copy.wait_send()

    return kernel


def solution(mesh):
    series_axis = mesh.shape["series"]
    torus = Mesh(mesh.devices.reshape(8, 8, 2, series_axis // 2, 2), AXES)
    sizes = dict(torus.shape)
    n_y, n_z = sizes["y"], sizes["z"]

    def local(returns, sector):
        time_rows, series = returns.shape
        half = time_rows // 2
        chunks = series // CHUNK
        f32 = jnp.float32
        dma = pltpu.SemaphoreType.DMA
        variance, pooled = pl.pallas_call(
            make_kernel(sizes, time_rows, series),
            name="rolling",
            out_shape=(
                jax.ShapeDtypeStruct((time_rows, series), f32),
                jax.ShapeDtypeStruct((1, series), f32),
            ),
            in_specs=[
                pl.BlockSpec(memory_space=pl.ANY),
                pl.BlockSpec(memory_space=pltpu.VMEM),
            ],
            out_specs=(
                pl.BlockSpec(memory_space=pl.ANY),
                pl.BlockSpec(memory_space=pltpu.VMEM),
            ),
            scratch_shapes=[
                pltpu.VMEM((time_rows + W, series), f32),
                pltpu.VMEM((time_rows + W, series), f32),
                pltpu.VMEM((SECTORS, series), jnp.bfloat16),
                pltpu.VMEM((half + COUNT_ROWS, SECTORS), f32),
                pltpu.VMEM((half + COUNT_ROWS, SECTORS), f32),
                pltpu.VMEM((half + COUNT_ROWS, SECTORS), f32),
                pltpu.VMEM((half + COUNT_ROWS, SECTORS), f32),
                pltpu.VMEM((time_rows, SECTORS), f32),
                pltpu.VMEM((W, SECTORS), f32),
                pltpu.VMEM((time_rows, series), f32),
                pltpu.VMEM((8, series), f32),
                pltpu.VMEM((8, 8, SECTORS), f32),
                pltpu.VMEM((n_y, 8, SECTORS), f32),
                pltpu.VMEM((n_z, 8, SECTORS), f32),
                dma((2,)),
                dma((chunks,)),
                dma((chunks,)),
                dma((3,)),
                dma((3,)),
                dma((2,)),
                dma((2,)),
                dma((2, chunks)),
                dma((8,)),
                dma((8,)),
                dma((n_y,)),
                dma((n_y,)),
                dma((n_z,)),
                dma((n_z,)),
            ],
            compiler_params=pltpu.CompilerParams(
                collective_id=0, has_side_effects=True, vmem_limit_bytes=56 * 2**20
            ),
        )(returns, sector[None, :])
        return variance + pooled

    return jax.shard_map(
        local,
        mesh=torus,
        in_specs=(P(("y", "z", "xh"), ("xl", "c")), P(("xl", "c"))),
        out_specs=P(("y", "z", "xh"), ("xl", "c")),
        check_vma=False,
    )
```

time: 154 us -> 62.6 us (0.41)
  Pallas kernels: 0 us -> 59.2 us
  blocking collectives: 48.7 us -> 0 us
  waiting for transfers between devices: 40.9 us -> 0 us
  matrix products: 25 us -> 0 us
  other arithmetic: 21 us -> 3.19 us
  starting transfers between devices: 11 us -> 0 us
  local copies, waits for them, and re-layouts: 6.67 us -> 0 us
    pallas_call x0 -> x1, Pallas kernels: none -> 59.2 us  [local(): pl.pallas_call(make_kernel(sizes, time_rows, series), name='rolling', out...]
    psum x3 -> x0, blocking collectives: 41.9 us -> none  [over_axes(): return functools.reduce(lax.psum, axes, array)]
    ppermute x2 -> x0, waiting for transfers between devices: 40.9 us -> none  [shifted(): lax.ppermute(value, axis, [(source, source + steps) for source in range(l...]
    dot_general x6 -> x0, matrix products: 25 us -> none  [the longest x1 12.1 us: window_variance(): jnp.dot(band_matrix(rows), stacked, precision=highest, preferred_element_...]
    reduce_sum x4 -> x0, other arithmetic: 8.27 us -> none  [the longest x2 5.46 us: taken_together(): return from_everyone(array, axis).sum(axis=0)]
    unnamed x4 -> x0, other arithmetic: 7.56 us -> none
    all_to_all x1 -> x0, blocking collectives: 6.79 us -> none  [from_everyone(): lax.all_to_all(jnp.broadcast_to(array[None], (size, *array.shape)), axis,...]
    ppermute x2 -> x0, starting transfers between devices: 6.32 us -> none  [shifted(): lax.ppermute(value, axis, [(source, source + steps) for source in range(l...]
  transfers between devices with their start and end apart: 3 -> 0, of which waited for: 2 -> 0; matrix products, arithmetic and copies ran while one was open for 3% -> 0% of each run, Pallas kernels for 0% -> 0%
where the time goes in v1:
time: 62.6 us; the launch traced here: 62.4 us
  Pallas kernels  59.2 us (95%)
  other arithmetic  3.19 us (5%)
    pallas_call x1, Pallas kernels, local(): pl.pallas_call(make_kernel(sizes, time_rows, series), name='rolling', out...  59.2 us
    add x1, other arithmetic, local(): return variance + pooled  3.19 us

profile of v1, /device:TPU:4, one launch (start us, length us, event | category | flops | bytes accessed | tf_op | source)
XLA Modules:
  0.0 62.4 jit_solution(4130990976464158845)
XLA Ops:
  0.0 59.2 %rolling.1 = (f32[256,2048]{1,0:T(8,128)}, f32[1,2048]{1,0:T(1,128)}) custom-call(f32[256,2048]{1,0:T(8,128)} %ret_hbm.1, s32[1,2048]{1,0:T(1,128)} %bitcast.2), custom_call_target="tpu_custom_call" | custom-call | tf_op jit(solution)/shard_map/rolling/pallas_call | solution.py:370
  59.2 3.2 %broadcast_add_fusion = f32[256,2048]{1,0:T(8,128)} fusion(f32[256,2048]{1,0:T(8,128)} %get-tuple-element.7, f32[2048]{0:T(1024)} %bitcast.3), kind=kLoop, calls=%fused_computation | loop fusion | flops 524288 | bytes 4202496 | tf_op jit(solution)/shard_map/add | solution.py:419

commit v2 on v1

v2 whole, which is shorter than its diff:
```python
import jax
import jax.numpy as jnp
from jax import lax
from jax.experimental import pallas as pl
from jax.experimental.pallas import tpu as pltpu
from jax.sharding import Mesh
from jax.sharding import PartitionSpec as P

W = 64
SECTORS = 512
AXES = ("y", "z", "xh", "xl", "c")
MESH_IDS = pl.DeviceIdType.MESH

ridge_rate = 0.05
shrink_weight = 0.3

LANES = 128
COUNT_ROWS = 8
CHUNK = 256
GROUPS = CHUNK // LANES
DEPTH = 512
KEPT = 3
PARTS = 2
EARLY = 2
MIDDLE = 4


def split3(value):
    hi = value.astype(jnp.bfloat16)
    rest = value - hi.astype(jnp.float32)
    mid = rest.astype(jnp.bfloat16)
    lo = (rest - mid.astype(jnp.float32)).astype(jnp.bfloat16)
    return hi, mid, lo


def split2(value):
    hi = value.astype(jnp.bfloat16)
    return hi, (value - hi.astype(jnp.float32)).astype(jnp.bfloat16)


def nn(a, b):
    return jnp.dot(a, b, preferred_element_type=jnp.float32)


def nt(a, b):
    return lax.dot_general(
        a, b, (((1,), (1,)), ((), ())), preferred_element_type=jnp.float32
    )


def eight(q):
    return pl.ds(8 * q, 8)


def spread(tile, run, pitch=8):
    per = run // 8
    return pl.ds(8 * pitch * (tile % per) + tile // per, 8, stride=pitch)


def kept(q, k):
    return pl.ds(KEPT * 8 * q + 8 * k, 8)


def carried(total, back):
    out = pltpu.roll(total, 1, 0)
    for j in range(2, back + 1):
        out = out + pltpu.roll(total, j, 0)
    return out


def totals_of(terms, run):
    total = terms(0)
    for q in range(1, run):
        total = [a + b for a, b in zip(total, terms(q))]
    return total


def slide(windows, terms, back):
    return [s + (v - pltpu.roll(v, back, 0)) for s, v in zip(windows, terms)]


def remote(src, dst, send, recv, device):
    return pltpu.make_async_remote_copy(
        src_ref=src,
        dst_ref=dst,
        send_sem=send,
        recv_sem=recv,
        device_id=device,
        device_id_type=MESH_IDS,
    )


def make_kernel(sizes, time_rows, series):
    n_y, n_z = sizes["y"], sizes["z"]
    half = time_rows // 2
    chunks = series // CHUNK
    tail = W // 2
    run = time_rows // 8
    back = W // run
    edge = 2 * W
    edge_run = edge // 8
    edge_back = W // edge_run

    def kernel(
        ret_hbm,
        sector_hbm,
        var,
        pooled_ref,
        sector,
        ret,
        keep,
        table,
        part,
        mine,
        from_core,
        from_pair,
        means,
        prior,
        spreader,
        mean_parts,
        edge_parts,
        fac_a,
        fac_b,
        fac_edge,
        work,
        ret_edge,
        edge_steps,
        col,
        sums,
        gx,
        gy,
        gz,
        load_sem,
        halo_send,
        halo_recv,
        ex_send,
        ex_recv,
        pm_send,
        pm_recv,
        gx_send,
        gx_recv,
        gy_send,
        gy_recv,
        gz_send,
        gz_recv,
    ):
        loads = [
            pltpu.make_async_copy(sector_hbm, sector, load_sem.at[2]),
            pltpu.make_async_copy(
                ret_hbm.at[time_rows - W :], ret.at[time_rows:], load_sem.at[0]
            ),
            pltpu.make_async_copy(
                ret_hbm.at[: time_rows - W], ret.at[W:time_rows], load_sem.at[1]
            ),
        ]
        for load in loads:
            load.start()

        y, z = lax.axis_index("y"), lax.axis_index("z")
        xh, xl, c = lax.axis_index("xh"), lax.axis_index("xl"), lax.axis_index("c")
        block = (y * n_z + z) * 2 + xh
        n_blocks = n_y * n_z * 2

        def place(b):
            b = lax.rem(b + n_blocks, n_blocks)
            return {"y": b // (2 * n_z), "z": lax.rem(b // 2, n_z), "xh": lax.rem(b, 2)}

        following, previous = place(block + 1), place(block - 1)
        core = {"c": 1 - c}
        pair = {"xl": 1 - xl}

        def x_peer(d):
            p = lax.rem(xh * 4 + xl * 2 + c + d, 8)
            return {"xh": p // 4, "xl": lax.rem(p // 2, 2), "c": lax.rem(p, 2)}

        def y_peer(d):
            return {"y": lax.rem(y + d, n_y)}

        def z_peer(d):
            return {"z": lax.rem(z + d, n_z)}

        peers = [following, previous]
        peers += [x_peer(d) for d in range(1, 8)]
        peers += [y_peer(d) for d in range(1, n_y)]
        peers += [z_peer(d) for d in range(1, n_z)]
        barrier = pltpu.get_barrier_semaphore()
        for peer in peers:
            pl.semaphore_signal(barrier, inc=1, device_id=peer, device_id_type=MESH_IDS)

        loads[0].wait()

        @pl.loop(0, chunks)
        def _(i):
            at = pl.multiple_of(i * CHUNK, CHUNK)
            labels = lax.broadcasted_iota(jnp.int32, (SECTORS, CHUNK), 0)
            hit = labels == sector[:, pl.ds(at, CHUNK)]
            table[:, pl.ds(at, CHUNK)] = hit.astype(jnp.float32).astype(jnp.bfloat16)

        loads[1].wait()
        pl.semaphore_wait(barrier, len(peers))

        def halo(i):
            at = pl.multiple_of(i * CHUNK, CHUNK)
            return remote(
                ret.at[time_rows:, pl.ds(at, CHUNK)],
                ret.at[:W, pl.ds(at, CHUNK)],
                halo_send.at[i],
                halo_recv.at[i],
                following,
            )

        for i in range(EARLY):
            halo(i).start()
        loads[2].wait()

        def columns(h):
            return pl.ds(h * (SECTORS // PARTS), SECTORS // PARTS)

        def partial_sums(which, into, h):
            first = pl.multiple_of(W + which * half, W)
            into[h] = jnp.zeros(into.shape[1:], jnp.float32)

            @pl.loop(0, series // DEPTH)
            def _(i):
                cols = pl.ds(pl.multiple_of(i * DEPTH, DEPTH), DEPTH)
                hi, lo = split2(ret[pl.ds(first, half), cols])
                ones = jnp.ones((2 * COUNT_ROWS, DEPTH), jnp.bfloat16)
                got = nt(jnp.concatenate([hi, lo, ones], axis=0), table[columns(h), cols])
                into[h, :half] += got[:half] + got[half : 2 * half]
                into[h, half:] += got[2 * half : 2 * half + COUNT_ROWS]

        to_core = [
            remote(part.at[h], from_core.at[h], ex_send.at[0, h], ex_recv.at[0, h], core)
            for h in range(PARTS)
        ]
        to_pair = [
            remote(mine.at[h], from_pair.at[h], ex_send.at[1, h], ex_recv.at[1, h], pair)
            for h in range(PARTS)
        ]
        for h in range(PARTS):
            partial_sums(1 - c, part, h)
            to_core[h].start()
        for h in range(PARTS):
            partial_sums(c, mine, h)
            to_core[h].wait_recv()
            mine[h] = mine[h] + from_core[h]
            to_pair[h].start()
        for i in range(EARLY, MIDDLE):
            halo(i).start()

        full = float(W)

        @pl.loop(0, series // LANES)
        def _(g):
            lanes = pl.ds(pl.multiple_of(g * LANES, LANES), LANES)
            for tile in range(time_rows // 8):
                keep[g, spread(tile, run, 8 * KEPT), :] = ret[
                    pl.ds(W + 8 * tile, 8), lanes
                ]

            def terms(q):
                r = keep[g, kept(q, 0), :]
                return [r, r * r]

            windows = [carried(t, back) for t in totals_of(terms, run)]
            for q in range(run):
                windows = slide(windows, terms(q), back)
                keep[g, kept(q, 1), :] = windows[0]
                keep[g, kept(q, 2), :] = windows[1] - windows[0] * (
                    windows[0] * (1.0 / full)
                )

        place_in = lax.broadcasted_iota(jnp.int32, (8, LANES), 0)
        for q in range(edge_run):
            seen = (place_in - edge_back) * edge_run + q + 1 + block * time_rows
            steps = jnp.minimum(jnp.maximum(seen, 1), W).astype(jnp.float32)
            edge_steps[0, eight(q), :] = 1.0 / steps
            edge_steps[1, eight(q), :] = ridge_rate * steps

        own = pl.ds(pl.multiple_of(c * half, half), half)
        share = [
            remote(
                means.at[own, columns(h)],
                means.at[own, columns(h)],
                ex_send.at[2, h],
                ex_recv.at[2, h],
                core,
            )
            for h in range(PARTS)
        ]
        counts = []
        for h in range(PARTS):
            to_pair[h].wait_recv()
            both = mine[h] + from_pair[h]
            counts.append(jnp.maximum(both[half : half + 1], 1.0))
            means[own, columns(h)] = both[:half] * (1.0 / counts[h])
            share[h].start()
        counts = jnp.concatenate(counts, axis=1)
        for h in range(PARTS):
            share[h].wait_recv()

        low = pl.multiple_of(c * tail, tail)
        pm_rows = prior.at[pl.ds(low, tail)]
        pm_on = remote(
            means.at[pl.ds(time_rows - W + low, tail)],
            pm_rows,
            pm_send.at[0],
            pm_recv.at[0],
            following,
        )
        pm_on.start()
        for i in range(MIDDLE, chunks):
            halo(i).start()

        for j in range(SECTORS // LANES):
            lanes = pl.ds(j * LANES, LANES)
            for tile in range(time_rows // 8):
                spreader[j, spread(tile, run), :] = means[eight(tile), lanes]
            for k, value in enumerate(split2(spreader[j])):
                mean_parts[k, :, lanes] = value

        def gathered(parts, i):
            hot = table[:, pl.ds(pl.multiple_of(i * CHUNK, CHUNK), CHUNK)]
            return nn(parts[0], hot) + nn(parts[1], hot)

        def interior(i, fac):
            for s in range(GROUPS):
                g = i * GROUPS + s
                lanes = pl.ds(pl.multiple_of(g * LANES, LANES), LANES)
                inner = pl.ds(s * LANES, LANES)

                def terms(q):
                    f = fac[eight(q), inner]
                    return [f, f * f, keep[g, kept(q, 0), :] * f]

                windows = [carried(t, back) for t in totals_of(terms, run)]
                total = jnp.zeros((8, LANES), jnp.float32)
                for q in range(run):
                    windows = slide(windows, terms(q), back)
                    mean_fac = windows[0] * (1.0 / full)
                    cff = windows[1] - windows[0] * mean_fac
                    crf = windows[2] - keep[g, kept(q, 1), :] * mean_fac
                    value = (
                        keep[g, kept(q, 2), :] - crf * crf / (cff + ridge_rate * full)
                    ) * (1.0 / full)
                    total = total + value
                    work[s, eight(q), :] = (1.0 - shrink_weight) * value
                col[:, lanes] = jnp.where(place_in >= back, total, 0.0)
                for tile in range(W // 8, time_rows // 8):
                    var[eight(tile), lanes] = work[s, spread(tile, run), :]

        fac_a[...] = gathered(mean_parts, 0)

        def two_chunks(j):
            fac_b[...] = gathered(mean_parts, 2 * j + 1)
            interior(2 * j, fac_a)
            fac_a[...] = gathered(mean_parts, lax.rem(2 * j + 2, chunks))
            interior(2 * j + 1, fac_b)

        pl.loop(0, chunks // 2 - 1)(two_chunks)
        pm_on.wait_recv()
        pm_share = remote(pm_rows, pm_rows, pm_send.at[1], pm_recv.at[1], core)
        pm_share.start()
        two_chunks(chunks // 2 - 1)
        pm_share.wait_recv()
        started = block > 0

        for j in range(SECTORS // LANES):
            lanes = pl.ds(j * LANES, LANES)
            for tile in range(edge // 8):
                if tile < W // 8:
                    value = jnp.where(started, prior[eight(tile), lanes], 0.0)
                else:
                    value = means[eight(tile - W // 8), lanes]
                spreader[j, spread(tile, edge_run), :] = value
            for k, value in enumerate(split2(spreader[j, :edge, :])):
                edge_parts[k, :, lanes] = value

        @pl.loop(0, chunks)
        def _(i):
            fac_edge[i] = gathered(edge_parts, i)

        late = place_in >= edge_back
        sums[...] = jnp.zeros_like(sums)

        @pl.loop(0, chunks)
        def _(i):
            halo(i).wait_recv()
            for s in range(GROUPS):
                lanes = pl.ds(pl.multiple_of(i * CHUNK + s * LANES, LANES), LANES)
                inner = pl.ds(s * LANES, LANES)
                for tile in range(edge // 8):
                    value = ret[eight(tile), lanes]
                    if tile < W // 8:
                        value = jnp.where(started, value, 0.0)
                    ret_edge[s, spread(tile, edge_run), :] = value

                def terms(q):
                    f = fac_edge[i, eight(q), inner]
                    r = ret_edge[s, eight(q), :]
                    return [r, r * r, f, f * f, r * f]

                windows = [carried(t, edge_back) for t in totals_of(terms, edge_run)]
                total = jnp.zeros((8, LANES), jnp.float32)
                for q in range(edge_run):
                    windows = slide(windows, terms(q), edge_back)
                    inv = edge_steps[0, eight(q), :]
                    s_r, s_rr, s_f, s_ff, s_rf = windows
                    mean_fac = s_f * inv
                    cff = s_ff - s_f * mean_fac
                    crf = s_rf - s_r * mean_fac
                    value = (
                        (s_rr - s_r * (s_r * inv))
                        - crf * crf / (cff + edge_steps[1, eight(q), :])
                    ) * inv
                    total = total + value
                    work[s, eight(q), :] = (1.0 - shrink_weight) * value
                col[:, lanes] += jnp.where(late, total, 0.0)
                for tile in range(W // 8, edge // 8):
                    var[eight(tile - W // 8), lanes] = work[s, spread(tile, edge_run), :]
            cols = pl.ds(pl.multiple_of(i * CHUNK, CHUNK), CHUNK)
            hot = table[:, cols]
            got = nt(jnp.concatenate(split3(col[:, cols]), axis=0), hot)
            sums[...] += got[0:8] + got[8:16] + got[16:24]

        def exchange(buf, peer_of, send, recv, count, total):
            buf[0] = jnp.broadcast_to(total, (8, SECTORS))
            copies = [
                remote(
                    buf.at[0, pl.ds(0, 1)],
                    buf.at[d, pl.ds(0, 1)],
                    send.at[d],
                    recv.at[d],
                    peer_of(d),
                )
                for d in range(1, count)
            ]
            for copy in copies:
                copy.start()
            for copy in copies:
                copy.wait_recv()
            total = buf[0, 0:1]
            for d in range(1, count):
                total = total + buf[d, 0:1]
            return total, copies

        total = jnp.sum(sums[...], axis=0, keepdims=True)
        total, x_copies = exchange(gx, x_peer, gx_send, gx_recv, 8, total)
        total, y_copies = exchange(gy, y_peer, gy_send, gy_recv, n_y, total)
        total, z_copies = exchange(gz, z_peer, gz_send, gz_recv, n_z, total)

        all_steps = float(time_rows * n_blocks)
        sector_mean = total / (all_steps * counts)
        parts = split3(jnp.broadcast_to(shrink_weight * sector_mean, (8, SECTORS)))
        got = nn(jnp.concatenate(parts, axis=0), table[...])
        pooled_ref[...] = got[0:1] + got[8:9] + got[16:17]

        for i in range(chunks):
            halo(i).wait_send()
        for copy in (*to_core, *to_pair, *share, pm_on, pm_share):
            copy.wait_send()
        for copy in x_copies + y_copies + z_copies:
            copy.wait_send()

    return kernel


def last_add(var, pooled, out, held, sems):
    rows = var.shape[0] // 4
    copies = []
    for i in range(4):
        block = pl.ds(i * rows, rows)
        held[block] = var[block] + pooled[...]
        copies.append(pltpu.make_async_copy(held.at[block], out.at[block], sems.at[i]))
        copies[-1].start()
    for copy in copies:
        copy.wait()


def solution(mesh):
    series_axis = mesh.shape["series"]
    torus = Mesh(mesh.devices.reshape(8, 8, 2, series_axis // 2, 2), AXES)
    sizes = dict(torus.shape)
    n_y, n_z = sizes["y"], sizes["z"]

    def local(returns, sector):
        time_rows, series = returns.shape
        half = time_rows // 2
        chunks = series // CHUNK
        groups = series // LANES
        f32, bf16 = jnp.float32, jnp.bfloat16
        dma = pltpu.SemaphoreType.DMA
        vmem = pltpu.VMEM
        variance, pooled = pl.pallas_call(
            make_kernel(sizes, time_rows, series),
            name="rolling",
            out_shape=(
                vmem((time_rows, series), f32),
                vmem((1, series), f32),
            ),
            in_specs=[pl.BlockSpec(memory_space=pltpu.HBM)] * 2,
            out_specs=(
                pl.BlockSpec(memory_space=pltpu.VMEM),
                pl.BlockSpec(memory_space=pltpu.VMEM),
            ),
            scratch_shapes=[
                vmem((1, series), jnp.int32),
                vmem((time_rows + W, series), f32),
                vmem((groups, KEPT * time_rows, LANES), f32),
                vmem((SECTORS, series), bf16),
                vmem((PARTS, half + COUNT_ROWS, SECTORS // PARTS), f32),
                vmem((PARTS, half + COUNT_ROWS, SECTORS // PARTS), f32),
                vmem((PARTS, half + COUNT_ROWS, SECTORS // PARTS), f32),
                vmem((PARTS, half + COUNT_ROWS, SECTORS // PARTS), f32),
                vmem((time_rows, SECTORS), f32),
                vmem((W, SECTORS), f32),
                vmem((SECTORS // LANES, time_rows, LANES), f32),
                vmem((2, time_rows, SECTORS), bf16),
                vmem((2, 2 * W, SECTORS), bf16),
                vmem((time_rows, CHUNK), f32),
                vmem((time_rows, CHUNK), f32),
                vmem((chunks, 2 * W, CHUNK), f32),
                vmem((GROUPS, time_rows, LANES), f32),
                vmem((GROUPS, 2 * W, LANES), f32),
                vmem((2, 2 * W, LANES), f32),
                vmem((8, series), f32),
                vmem((8, SECTORS), f32),
                vmem((8, 8, SECTORS), f32),
                vmem((n_y, 8, SECTORS), f32),
                vmem((n_z, 8, SECTORS), f32),
                dma((3,)),
                dma((chunks,)),
                dma((chunks,)),
                dma((3, PARTS)),
                dma((3, PARTS)),
                dma((2,)),
                dma((2,)),
                dma((8,)),
                dma((8,)),
                dma((n_y,)),
                dma((n_y,)),
                dma((n_z,)),
                dma((n_z,)),
            ],
            compiler_params=pltpu.CompilerParams(
                collective_id=0, has_side_effects=True, vmem_limit_bytes=48 * 2**20
            ),
        )(
            pltpu.with_memory_space_constraint(returns, pltpu.HBM),
            pltpu.with_memory_space_constraint(sector[None, :], pltpu.HBM),
        )
        return pl.pallas_call(
            last_add,
            name="last_add",
            out_shape=jax.ShapeDtypeStruct((time_rows, series), f32),
            in_specs=[pl.BlockSpec(memory_space=pltpu.VMEM)] * 2,
            out_specs=pl.BlockSpec(memory_space=pl.ANY),
            scratch_shapes=[vmem((time_rows, series), f32), dma((4,))],
            compiler_params=pltpu.CompilerParams(vmem_limit_bytes=8 * 2**20),
        )(variance, pooled)

    return jax.shard_map(
        local,
        mesh=torus,
        in_specs=(P(("y", "z", "xh"), ("xl", "c")), P(("xl", "c"))),
        out_specs=P(("y", "z", "xh"), ("xl", "c")),
        check_vma=False,
    )
```

time: 62.6 us -> 55.8 us (0.89)
  Pallas kernels: 59.2 us -> 55.7 us
  other arithmetic: 3.19 us -> 0 us
    pallas_call x1, Pallas kernels: 59.2 us -> 54.3 us  [local(): pl.pallas_call(make_kernel(sizes, time_rows, series), name='rolling', out...]
    add x1 -> x0, other arithmetic: 3.19 us -> none  [local(): return variance + pooled]
    pallas_call x0 -> x1, Pallas kernels: none -> 1.38 us  [local(): pl.pallas_call(last_add, name='last_add', out_shape=jax.ShapeDtypeStruct(...]
where the time goes in v2:
time: 55.8 us; the launch traced here: 55.7 us
  Pallas kernels  55.7 us (100%)
    pallas_call x1, Pallas kernels, local(): pl.pallas_call(make_kernel(sizes, time_rows, series), name='rolling', out...  54.3 us
    pallas_call x1, Pallas kernels, local(): pl.pallas_call(last_add, name='last_add', out_shape=jax.ShapeDtypeStruct(...  1.38 us

profile of v2, /device:TPU:4, one launch (start us, length us, event | category | flops | bytes accessed | tf_op | source)
XLA Modules:
  0.0 55.7 jit_solution(16455697739478809295)
XLA Ops:
  0.0 54.3 %rolling.1 = (f32[256,2048]{1,0:T(8,128)S(1)}, f32[1,2048]{1,0:T(1,128)S(1)}) custom-call(f32[256,2048]{1,0:T(8,128)} %ret_hbm.1, s32[1,2048]{1,0:T(1,128)} %bitcast.1), custom_call_target="tpu_custom_call" | custom-call | tf_op jit(solution)/shard_map/rolling/pallas_call | solution.py:494
  54.3 1.4 %last_add.1 = f32[256,2048]{1,0:T(8,128)} custom-call(f32[256,2048]{1,0:T(8,128)S(1)} %get-tuple-element.7.var, f32[1,2048]{1,0:T(1,128)S(1)} %get-tuple-element.8.pooled), custom_call_target="tpu_custom_call" | custom-call | tf_op jit(solution)/shard_map/last_add/pallas_call | solution.py:552

commit v3 on v2

--- a/solution.py
+++ b/solution.py
@@ -23,6 +23,8 @@
 PARTS = 2
 EARLY = 2
 MIDDLE = 4
+BATCH = 4
+LAST = 2
 
 
 def split3(value):
@@ -119,8 +121,7 @@
         spreader,
         mean_parts,
         edge_parts,
-        fac_a,
-        fac_b,
+        fac,
         fac_edge,
         work,
         ret_edge,
@@ -218,16 +219,15 @@
 
         def partial_sums(which, into, h):
             first = pl.multiple_of(W + which * half, W)
-            into[h] = jnp.zeros(into.shape[1:], jnp.float32)
-
-            @pl.loop(0, series // DEPTH)
-            def _(i):
-                cols = pl.ds(pl.multiple_of(i * DEPTH, DEPTH), DEPTH)
+            ones = jnp.ones((2 * COUNT_ROWS, DEPTH), jnp.bfloat16)
+            got = None
+            for at in range(0, series, DEPTH):
+                cols = pl.ds(at, DEPTH)
                 hi, lo = split2(ret[pl.ds(first, half), cols])
-                ones = jnp.ones((2 * COUNT_ROWS, DEPTH), jnp.bfloat16)
-                got = nt(jnp.concatenate([hi, lo, ones], axis=0), table[columns(h), cols])
-                into[h, :half] += got[:half] + got[half : 2 * half]
-                into[h, half:] += got[2 * half : 2 * half + COUNT_ROWS]
+                more = nt(jnp.concatenate([hi, lo, ones], axis=0), table[columns(h), cols])
+                got = more if got is None else got + more
+            into[h, :half] = got[:half] + got[half : 2 * half]
+            into[h, half:] = got[2 * half : 2 * half + COUNT_ROWS]
 
         to_core = [
             remote(part.at[h], from_core.at[h], ex_send.at[0, h], ex_recv.at[0, h], core)
@@ -323,14 +323,14 @@
             hot = table[:, pl.ds(pl.multiple_of(i * CHUNK, CHUNK), CHUNK)]
             return nn(parts[0], hot) + nn(parts[1], hot)
 
-        def interior(i, fac):
+        def interior(i):
             for s in range(GROUPS):
                 g = i * GROUPS + s
                 lanes = pl.ds(pl.multiple_of(g * LANES, LANES), LANES)
                 inner = pl.ds(s * LANES, LANES)
 
                 def terms(q):
-                    f = fac[eight(q), inner]
+                    f = fac[i, eight(q), inner]
                     return [f, f * f, keep[g, kept(q, 0), :] * f]
 
                 windows = [carried(t, back) for t in totals_of(terms, run)]
@@ -349,19 +349,16 @@
                 for tile in range(W // 8, time_rows // 8):
                     var[eight(tile), lanes] = work[s, spread(tile, run), :]
 
-        fac_a[...] = gathered(mean_parts, 0)
-
-        def two_chunks(j):
-            fac_b[...] = gathered(mean_parts, 2 * j + 1)
-            interior(2 * j, fac_a)
-            fac_a[...] = gathered(mean_parts, lax.rem(2 * j + 2, chunks))
-            interior(2 * j + 1, fac_b)
-
-        pl.loop(0, chunks // 2 - 1)(two_chunks)
+        @pl.loop(0, chunks // BATCH)
+        def _(i):
+            for b in range(BATCH):
+                fac[i * BATCH + b] = gathered(mean_parts, i * BATCH + b)
+
+        pl.loop(0, chunks - LAST)(interior)
         pm_on.wait_recv()
         pm_share = remote(pm_rows, pm_rows, pm_send.at[1], pm_recv.at[1], core)
         pm_share.start()
-        two_chunks(chunks // 2 - 1)
+        pl.loop(chunks - LAST, chunks)(interior)
         pm_share.wait_recv()
         started = block > 0
 
@@ -376,15 +373,14 @@
             for k, value in enumerate(split2(spreader[j, :edge, :])):
                 edge_parts[k, :, lanes] = value
 
-        @pl.loop(0, chunks)
+        @pl.loop(0, chunks // BATCH)
         def _(i):
-            fac_edge[i] = gathered(edge_parts, i)
+            for b in range(BATCH):
+                fac_edge[i * BATCH + b] = gathered(edge_parts, i * BATCH + b)
 
         late = place_in >= edge_back
-        sums[...] = jnp.zeros_like(sums)
-
-        @pl.loop(0, chunks)
-        def _(i):
+
+        def boundary(i):
             halo(i).wait_recv()
             for s in range(GROUPS):
                 lanes = pl.ds(pl.multiple_of(i * CHUNK + s * LANES, LANES), LANES)
@@ -418,10 +414,16 @@
                 col[:, lanes] += jnp.where(late, total, 0.0)
                 for tile in range(W // 8, edge // 8):
                     var[eight(tile - W // 8), lanes] = work[s, spread(tile, edge_run), :]
-            cols = pl.ds(pl.multiple_of(i * CHUNK, CHUNK), CHUNK)
-            hot = table[:, cols]
-            got = nt(jnp.concatenate(split3(col[:, cols]), axis=0), hot)
-            sums[...] += got[0:8] + got[8:16] + got[16:24]
+
+        def sector_sums(first, last):
+            cols = pl.ds(first * CHUNK, (last - first) * CHUNK)
+            got = nt(jnp.concatenate(split3(col[:, cols]), axis=0), table[:, cols])
+            return got[0:8] + got[8:16] + got[16:24]
+
+        pl.loop(0, chunks - LAST)(boundary)
+        sums[...] = sector_sums(0, chunks - LAST)
+        pl.loop(chunks - LAST, chunks)(boundary)
+        sums[...] += sector_sums(chunks - LAST, chunks)
 
         def exchange(buf, peer_of, send, recv, count, total):
             buf[0] = jnp.broadcast_to(total, (8, SECTORS))
@@ -517,8 +519,7 @@
                 vmem((SECTORS // LANES, time_rows, LANES), f32),
                 vmem((2, time_rows, SECTORS), bf16),
                 vmem((2, 2 * W, SECTORS), bf16),
-                vmem((time_rows, CHUNK), f32),
-                vmem((time_rows, CHUNK), f32),
+                vmem((chunks, time_rows, CHUNK), f32),
                 vmem((chunks, 2 * W, CHUNK), f32),
                 vmem((GROUPS, time_rows, LANES), f32),
                 vmem((GROUPS, 2 * W, LANES), f32),

time: 55.8 us -> 55.5 us (level)
  no operation moved by 1% of the time
where the time goes in v3:
time: 55.5 us; the launch traced here: 55.4 us
  Pallas kernels  55.4 us (100%)
    pallas_call x1, Pallas kernels, local(): pl.pallas_call(make_kernel(sizes, time_rows, series), name='rolling', out...  54 us
    pallas_call x1, Pallas kernels, local(): pl.pallas_call(last_add, name='last_add', out_shape=jax.ShapeDtypeStruct(...  1.38 us

profile of v3, /device:TPU:4, one launch (start us, length us, event | category | flops | bytes accessed | tf_op | source)
XLA Modules:
  0.0 55.4 jit_solution(1216082549111961251)
XLA Ops:
  0.0 54.0 %rolling.1 = (f32[256,2048]{1,0:T(8,128)S(1)}, f32[1,2048]{1,0:T(1,128)S(1)}) custom-call(f32[256,2048]{1,0:T(8,128)} %ret_hbm.1, s32[1,2048]{1,0:T(1,128)} %bitcast.1), custom_call_target="tpu_custom_call" | custom-call | tf_op jit(solution)/shard_map/rolling/pallas_call | solution.py:496
  54.0 1.4 %last_add.1 = f32[256,2048]{1,0:T(8,128)} custom-call(f32[256,2048]{1,0:T(8,128)S(1)} %get-tuple-element.7.var, f32[1,2048]{1,0:T(1,128)S(1)} %get-tuple-element.8.pooled), custom_call_target="tpu_custom_call" | custom-call | tf_op jit(solution)/shard_map/last_add/pallas_call | solution.py:553

commit v4 on v3

--- a/solution.py
+++ b/solution.py
@@ -22,7 +22,7 @@
 KEPT = 3
 PARTS = 2
 EARLY = 2
-MIDDLE = 4
+MIDDLE = 3
 BATCH = 4
 LAST = 2
 
@@ -97,6 +97,7 @@
     half = time_rows // 2
     chunks = series // CHUNK
     tail = W // 2
+    body = half - tail
     run = time_rows // 8
     back = W // run
     edge = 2 * W
@@ -218,12 +219,16 @@
             return pl.ds(h * (SECTORS // PARTS), SECTORS // PARTS)
 
         def partial_sums(which, into, h):
-            first = pl.multiple_of(W + which * half, W)
+            first = pl.multiple_of(W + which * body, tail)
+            last = pl.multiple_of(time_rows + which * tail, tail)
             ones = jnp.ones((2 * COUNT_ROWS, DEPTH), jnp.bfloat16)
             got = None
             for at in range(0, series, DEPTH):
                 cols = pl.ds(at, DEPTH)
-                hi, lo = split2(ret[pl.ds(first, half), cols])
+                rows = jnp.concatenate(
+                    [ret[pl.ds(first, body), cols], ret[pl.ds(last, tail), cols]], axis=0
+                )
+                hi, lo = split2(rows)
                 more = nt(jnp.concatenate([hi, lo, ones], axis=0), table[columns(h), cols])
                 got = more if got is None else got + more
             into[h, :half] = got[:half] + got[half : 2 * half]
@@ -245,9 +250,6 @@
             to_core[h].wait_recv()
             mine[h] = mine[h] + from_core[h]
             to_pair[h].start()
-        for i in range(EARLY, MIDDLE):
-            halo(i).start()
-
         full = float(W)
 
         @pl.loop(0, series // LANES)
@@ -277,14 +279,32 @@
             edge_steps[0, eight(q), :] = 1.0 / steps
             edge_steps[1, eight(q), :] = ridge_rate * steps
 
-        own = pl.ds(pl.multiple_of(c * half, half), half)
+        low = pl.multiple_of(c * tail, tail)
+        owned = (
+            pl.ds(pl.multiple_of(c * body, tail), body),
+            pl.ds(pl.multiple_of(time_rows - W + c * tail, tail), tail),
+        )
+        pm_rows = prior.at[pl.ds(low, tail)]
         share = [
+            [
+                remote(
+                    means.at[rows, columns(h)],
+                    means.at[rows, columns(h)],
+                    ex_send.at[2 + k, h],
+                    ex_recv.at[2 + k, h],
+                    core,
+                )
+                for k, rows in enumerate(owned)
+            ]
+            for h in range(PARTS)
+        ]
+        pm_on = [
             remote(
-                means.at[own, columns(h)],
-                means.at[own, columns(h)],
-                ex_send.at[2, h],
-                ex_recv.at[2, h],
-                core,
+                means.at[owned[1], columns(h)],
+                prior.at[pl.ds(low, tail), columns(h)],
+                pm_send.at[h],
+                pm_recv.at[h],
+                following,
             )
             for h in range(PARTS)
         ]
@@ -293,24 +313,18 @@
             to_pair[h].wait_recv()
             both = mine[h] + from_pair[h]
             counts.append(jnp.maximum(both[half : half + 1], 1.0))
-            means[own, columns(h)] = both[:half] * (1.0 / counts[h])
-            share[h].start()
+            scaled = both[:half] * (1.0 / counts[h])
+            means[owned[1], columns(h)] = scaled[body:]
+            means[owned[0], columns(h)] = scaled[:body]
+            pm_on[h].start()
+            for copy in share[h]:
+                copy.start()
+            for i in (range(EARLY, MIDDLE), range(MIDDLE, chunks))[h]:
+                halo(i).start()
         counts = jnp.concatenate(counts, axis=1)
         for h in range(PARTS):
-            share[h].wait_recv()
-
-        low = pl.multiple_of(c * tail, tail)
-        pm_rows = prior.at[pl.ds(low, tail)]
-        pm_on = remote(
-            means.at[pl.ds(time_rows - W + low, tail)],
-            pm_rows,
-            pm_send.at[0],
-            pm_recv.at[0],
-            following,
-        )
-        pm_on.start()
-        for i in range(MIDDLE, chunks):
-            halo(i).start()
+            for copy in share[h]:
+                copy.wait_recv()
 
         for j in range(SECTORS // LANES):
             lanes = pl.ds(j * LANES, LANES)
@@ -354,11 +368,12 @@
             for b in range(BATCH):
                 fac[i * BATCH + b] = gathered(mean_parts, i * BATCH + b)
 
-        pl.loop(0, chunks - LAST)(interior)
-        pm_on.wait_recv()
-        pm_share = remote(pm_rows, pm_rows, pm_send.at[1], pm_recv.at[1], core)
+        pl.loop(0, chunks // 2)(interior)
+        for copy in pm_on:
+            copy.wait_recv()
+        pm_share = remote(pm_rows, pm_rows, pm_send.at[2], pm_recv.at[2], core)
         pm_share.start()
-        pl.loop(chunks - LAST, chunks)(interior)
+        pl.loop(chunks // 2, chunks)(interior)
         pm_share.wait_recv()
         started = block > 0
 
@@ -459,7 +474,7 @@
 
         for i in range(chunks):
             halo(i).wait_send()
-        for copy in (*to_core, *to_pair, *share, pm_on, pm_share):
+        for copy in (*to_core, *to_pair, *share[0], *share[1], *pm_on, pm_share):
             copy.wait_send()
         for copy in x_copies + y_copies + z_copies:
             copy.wait_send()
@@ -532,10 +547,10 @@
                 dma((3,)),
                 dma((chunks,)),
                 dma((chunks,)),
-                dma((3, PARTS)),
-                dma((3, PARTS)),
-                dma((2,)),
-                dma((2,)),
+                dma((4, PARTS)),
+                dma((4, PARTS)),
+                dma((3,)),
+                dma((3,)),
                 dma((8,)),
                 dma((8,)),
                 dma((n_y,)),

time: 55.5 us -> 59.3 us (1.068)
  Pallas kernels: 55.4 us -> 59.1 us
    pallas_call x1, Pallas kernels: 54 us -> 57.7 us  [local(): pl.pallas_call(make_kernel(sizes, time_rows, series), name='rolling', out...]
where the time goes in v4:
time: 59.3 us; the launch traced here: 59.1 us
  Pallas kernels  59.1 us (100%)
    pallas_call x1, Pallas kernels, local(): pl.pallas_call(make_kernel(sizes, time_rows, series), name='rolling', out...  57.7 us
    pallas_call x1, Pallas kernels, local(): pl.pallas_call(last_add, name='last_add', out_shape=jax.ShapeDtypeStruct(...  1.38 us

profile of v4, /device:TPU:4, one launch (start us, length us, event | category | flops | bytes accessed | tf_op | source)
XLA Modules:
  0.0 59.1 jit_solution(11362580782999896233)
XLA Ops:
  0.0 57.7 %rolling.1 = (f32[256,2048]{1,0:T(8,128)S(1)}, f32[1,2048]{1,0:T(1,128)S(1)}) custom-call(f32[256,2048]{1,0:T(8,128)} %ret_hbm.1, s32[1,2048]{1,0:T(1,128)} %bitcast.1), custom_call_target="tpu_custom_call" | custom-call | tf_op jit(solution)/shard_map/rolling/pallas_call | solution.py:511
  57.8 1.4 %last_add.1 = f32[256,2048]{1,0:T(8,128)} custom-call(f32[256,2048]{1,0:T(8,128)S(1)} %get-tuple-element.7.var, f32[1,2048]{1,0:T(1,128)S(1)} %get-tuple-element.8.pooled), custom_call_target="tpu_custom_call" | custom-call | tf_op jit(solution)/shard_map/last_add/pallas_call | solution.py:568

commit v5 on v4

--- a/solution.py
+++ b/solution.py
@@ -22,7 +22,7 @@
 KEPT = 3
 PARTS = 2
 EARLY = 2
-MIDDLE = 3
+MIDDLE = 4
 BATCH = 4
 LAST = 2
 
@@ -250,6 +250,8 @@
             to_core[h].wait_recv()
             mine[h] = mine[h] + from_core[h]
             to_pair[h].start()
+        for i in range(EARLY, MIDDLE):
+            halo(i).start()
         full = float(W)
 
         @pl.loop(0, series // LANES)
@@ -316,15 +318,15 @@
             scaled = both[:half] * (1.0 / counts[h])
             means[owned[1], columns(h)] = scaled[body:]
             means[owned[0], columns(h)] = scaled[:body]
-            pm_on[h].start()
             for copy in share[h]:
                 copy.start()
-            for i in (range(EARLY, MIDDLE), range(MIDDLE, chunks))[h]:
-                halo(i).start()
+            pm_on[h].start()
         counts = jnp.concatenate(counts, axis=1)
         for h in range(PARTS):
             for copy in share[h]:
                 copy.wait_recv()
+        for i in range(MIDDLE, chunks):
+            halo(i).start()
 
         for j in range(SECTORS // LANES):
             lanes = pl.ds(j * LANES, LANES)

time: 59.3 us -> 54.9 us (0.926)
  Pallas kernels: 59.1 us -> 54.7 us
    pallas_call x1, Pallas kernels: 57.7 us -> 53.4 us  [local(): pl.pallas_call(make_kernel(sizes, time_rows, series), name='rolling', out...]
where the time goes in v5:
time: 54.9 us; the launch traced here: 54.7 us
  Pallas kernels  54.7 us (100%)
    pallas_call x1, Pallas kernels, local(): pl.pallas_call(make_kernel(sizes, time_rows, series), name='rolling', out...  53.4 us
    pallas_call x1, Pallas kernels, local(): pl.pallas_call(last_add, name='last_add', out_shape=jax.ShapeDtypeStruct(...  1.38 us

profile of v5, /device:TPU:4, one launch (start us, length us, event | category | flops | bytes accessed | tf_op | source)
XLA Modules:
  0.0 54.7 jit_solution(14615877558205471816)
XLA Ops:
  0.0 53.4 %rolling.1 = (f32[256,2048]{1,0:T(8,128)S(1)}, f32[1,2048]{1,0:T(1,128)S(1)}) custom-call(f32[256,2048]{1,0:T(8,128)} %ret_hbm.1, s32[1,2048]{1,0:T(1,128)} %bitcast.1), custom_call_target="tpu_custom_call" | custom-call | tf_op jit(solution)/shard_map/rolling/pallas_call | solution.py:513
  53.4 1.4 %last_add.1 = f32[256,2048]{1,0:T(8,128)} custom-call(f32[256,2048]{1,0:T(8,128)S(1)} %get-tuple-element.7.var, f32[1,2048]{1,0:T(1,128)S(1)} %get-tuple-element.8.pooled), custom_call_target="tpu_custom_call" | custom-call | tf_op jit(solution)/shard_map/last_add/pallas_call | solution.py:570
